TPU v7x, 256 devices: a whole 4x4x8 slice. The times are simulated.
256 devices in a mesh: grp: 8 (over x, core), dp: 32 (over y, z).
Axes of the slice: x: 4, y: 4, z: 8, core: 2. Of those that a mesh axis runs over, the one named last changes fastest.
Arguments:
- chosen_ids: int32 [256, 512], P(('grp', 'dp')), may hold values from 0 to 128255, as said below
- rejected_ids: int32 [256, 512], P(('grp', 'dp')), may hold values from 0 to 128255, as said below
- chosen_len: int32 [256], P(('grp', 'dp')), may hold values from 64 to 256
- rejected_len: int32 [256], P(('grp', 'dp')), may hold values from 64 to 256
- chosen_logp: float32 [256, 512], P(('grp', 'dp')), may hold values from -0.3 to -0.01
- rejected_logp: float32 [256, 512], P(('grp', 'dp')), may hold values from -0.3 to -0.01
- ref_logp: float32 [2, 256], P(None, ('grp', 'dp')), may hold values from -40 to -10
- chosen_grads: bfloat16 [256, 512, 4096], P(('grp', 'dp')), may hold values from -48 to 48
- rejected_grads: bfloat16 [256, 512, 4096], P(('grp', 'dp')), may hold values from -48 to 48
Outputs:
- grad_table: bfloat16 [128256, 4096], P(('grp', 'dp'))
Inputs may be any that keep to these rules, and one draw needn't show every extreme that they name: `chosen_ids`: vocabulary row v belongs to owner v // 501. The chosen and rejected tokens of one device's pairs together fall at most 6 times into one owner's rows; 16 owners drawn from the seed get exactly 6 of them from every device. `rejected_ids`: drawn together with chosen_ids under the same bound. The response is the last chosen_len[p] positions of the sequence. The response is the last rejected_len[p] positions of the sequence.
All inputs are finite; a program needn't handle non-finite values.
Results may differ from a plain program's by a relative error of at most 0.001.
The roundings to bfloat16 on the way count: a program that leaves them out, or rounds other values in their place, can miss the bound.
Values may be sent and summed in bfloat16 or wider, within the bound.
No kernel may reach another device: no remote copies, remote signals or barrier semaphores. Data moves between devices by JAX's collectives and lax.ppermute only.
A program may use at most 128 MiB of HBM per device.

v0:
```python
import jax
import jax.numpy as jnp
from jax import lax
from jax.sharding import PartitionSpec as P

VOCAB = 128256


beta_scale = 0.1


def in_blocks(array, dim, peers):
    before, after = (array.shape[:dim], array.shape[dim + 1 :])
    return jnp.moveaxis(array.reshape(*before, peers, -1, *after), dim, 0)


def joined_along(pieces, dim):
    pieces = jnp.moveaxis(pieces, 0, dim)
    lengths = pieces.shape
    return pieces.reshape(*lengths[:dim], lengths[dim] * lengths[dim + 1], *lengths[dim + 2 :])


def joined_exchange(array, axis, axes, splits, concats):
    sizes = [lax.axis_size(a) for a in axes]
    pieces = in_blocks(array, splits[0], sizes[0])
    pieces = jnp.moveaxis(in_blocks(pieces, splits[1] + 1, sizes[1]), 0, 1)
    inside = pieces.shape[2:]
    pieces = pieces.reshape(-1, *inside)
    pieces = lax.all_to_all(pieces, axis, split_axis=0, concat_axis=0, tiled=True)
    pieces = joined_along(pieces.reshape(*sizes, *inside), concats[0] + 1)
    return joined_along(pieces, concats[1])


def local(
    chosen_ids,
    rejected_ids,
    chosen_len,
    rejected_len,
    chosen_logp,
    rejected_logp,
    ref_logp,
    chosen_grads,
    rejected_grads,
):
    pair_count, seq_length = chosen_ids.shape
    feature_count = chosen_grads.shape[2]
    group_count = lax.axis_size("grp")
    member_count = lax.axis_size("dp")
    owner_total = group_count * member_count
    row_count = VOCAB // owner_total
    capacity = max(2, 3 * pair_count * seq_length // owner_total)
    positions = jnp.arange(seq_length)
    chosen_mask = (positions[None, :] >= seq_length - chosen_len[:, None]).astype(jnp.float32)
    rejected_mask = (positions[None, :] >= seq_length - rejected_len[:, None]).astype(jnp.float32)
    chosen_policy = jnp.sum(chosen_mask * chosen_logp, axis=1)
    rejected_policy = jnp.sum(rejected_mask * rejected_logp, axis=1)
    margin = beta_scale * (chosen_policy - ref_logp[0] - (rejected_policy - ref_logp[1]))
    pair_weight = beta_scale * jax.nn.sigmoid(-margin)
    chosen_rows = (-pair_weight[:, None, None] * chosen_grads.astype(jnp.float32)).astype(
        jnp.bfloat16
    )
    rejected_rows = (pair_weight[:, None, None] * rejected_grads.astype(jnp.float32)).astype(
        jnp.bfloat16
    )
    grad_rows = jnp.concatenate(
        [chosen_rows.reshape(-1, feature_count), rejected_rows.reshape(-1, feature_count)], axis=0
    )
    token_ids = jnp.concatenate([chosen_ids.reshape(-1), rejected_ids.reshape(-1)], axis=0)
    owner_index = token_ids // row_count
    local_row = token_ids - owner_index * row_count
    owner_hits = (owner_index[:, None] == jnp.arange(owner_total, dtype=jnp.int32)[None, :]).astype(
        jnp.int32
    )
    slot_rank = jnp.sum((jnp.cumsum(owner_hits, axis=0) - owner_hits) * owner_hits, axis=1)
    slot_index = owner_index * capacity + slot_rank
    outgoing = (
        jnp.zeros((owner_total * capacity, feature_count), jnp.bfloat16)
        .at[slot_index]
        .set(grad_rows)
    )
    slot_labels = (
        jnp.full((owner_total * capacity,), row_count, jnp.int32).at[slot_index].set(local_row)
    )
    label_pair = jnp.stack([slot_labels // 16, slot_labels % 16], axis=1).astype(jnp.bfloat16)
    outgoing = outgoing.reshape(group_count, member_count, capacity, feature_count)
    label_pair = label_pair.reshape(group_count, member_count, capacity, 2)
    arrived, label_in = (
        joined_exchange(outgoing, ("grp", "dp"), ("grp", "dp"), (0, 1), (0, 1)),
        joined_exchange(label_pair, ("grp", "dp"), ("grp", "dp"), (0, 1), (0, 1)),
    )
    label_in = label_in.reshape(-1, 2).astype(jnp.int32)
    arrived_rows = label_in[:, 0] * 16 + label_in[:, 1]
    arrived = arrived.reshape(-1, feature_count)
    selector = (jnp.arange(row_count, dtype=jnp.int32)[:, None] == arrived_rows[None, :]).astype(
        jnp.bfloat16
    )
    return jnp.dot(selector, arrived, preferred_element_type=jnp.float32).astype(jnp.bfloat16)


def solution(mesh):
    return jax.shard_map(
        local,
        mesh=mesh,
        in_specs=(
            P(("grp", "dp"), None),
            P(("grp", "dp"), None),
            P(("grp", "dp")),
            P(("grp", "dp")),
            P(("grp", "dp"), None),
            P(("grp", "dp"), None),
            P(None, ("grp", "dp")),
            P(("grp", "dp"), None, None),
            P(("grp", "dp"), None, None),
        ),
        out_specs=P(("grp", "dp"), None),
        check_vma=False,
    )
```

profile of v0, /device:TPU:1, one launch (start us, length us, event | category | flops | bytes accessed | tf_op | source)
XLA Modules:
  0.0 499.9 jit_solution(18231950029558250599)
XLA Ops:
  0.0 0.7 broadcast_divide_fusion
  0.7 0.7 fusion.22
  1.6 0.2 fusion.7
  1.9 0.3 copy.20
  2.3 0.7 multiply_subtract_fusion
  3.0 0.4 fusion.6
  3.4 0.7 compare_select_fusion
  4.1 4.3 scatter_custom_fusion
  8.4 0.2 stack.9
  8.6 0.2 stack.10
  8.8 0.8 copy.21
  9.6 15.7 %all-to-all-start = ((bf16[256,1,1,6,2]{3,4,2,1,0:T(2,128)(2,1)}), bf16[256,1,1,6,2]{3,4,2,1,0:T(2,128)(2,1)S(1)}, u32[]{:S(2)}, u32[]{:S(2)}) async-start(bf16[256,1,1,6,2]{3,4,2,1,0:T(2,128)(2,1)} %copy.21), calls=%async_computation | async-start | bytes 262144 | tf_op jit(solution)/shard_map/all_to_all | solution.py:29
  26.6 1.4 fusion.23
  28.0 1.3 fusion.21
  29.2 1.3 fusion.20
  33.1 9.3 %fusion.2 = (bf16[512,4096]{1,0:T(8,128)(2,1)}, bf16[512,4096]{1,0:T(8,128)(2,1)}) fusion(bf16[1,512,4096]{2,1,0:T(8,128)(2,1)} %param.16, f32[]{:T(128)} %bitcast.20, bf16[1,512,4096]{2,1,0:T(8,128)(2,1)} %param.17, f32[]{:T(128)} %bitcast.22), kind=kLoop, calls=%fused_computation.8 | loop fusion | flops 12582912 | bytes 16777224 | tf_op jit(solution)/shard_map/reshape | solution.py:66
  42.5 7.8 %pad_maximum_fusion = bf16[1024,4096]{1,0:T(8,128)(2,1)} fusion(bf16[512,4096]{1,0:T(8,128)(2,1)} %get-tuple-element.14, bf16[512,4096]{1,0:T(8,128)(2,1)} %get-tuple-element.13), kind=kLoop, calls=%fused_computation.2 | loop fusion | flops 16777216 | bytes 16777216 | tf_op jit(solution)/shard_map/concatenate | solution.py:65
  50.2 19.9 %scatter_custom_fusion.1 = bf16[1536,4096]{1,0:T(8,128)(2,1)} fusion(s32[1024]{0:T(1024)S(1)} %bitcast.71, bf16[1024,4096]{1,0:T(8,128)(2,1)} %pad_maximum_fusion, bf16[]{:T(256)} %constant.58.clone.1), kind=kCustom, calls=%fused_computation.5 | custom fusion | bytes 12583424 | tf_op jit(solution)/shard_map/scatter | solution.py:79
  70.1 18.5 %reshape_transpose_transpose_reshape_reshape_reshape.4 = bf16[256,1,1,6,4096]{4,3,0,2,1:T(8,128)(2,1)} reshape(bf16[1536,4096]{1,0:T(8,128)(2,1)} %scatter_custom_fusion.1) | data formatting | bytes 25165824 | tf_op jit(solution)/shard_map/reshape;transpose;transpose;reshape;reshape;reshape | solution.py:28
  88.7 14.7 %all-to-all-start.1 = ((bf16[256,1,1,6,4096]{4,3,2,1,0:T(8,128)(2,1)}), bf16[256,1,1,6,4096]{4,3,2,1,0:T(8,128)(2,1)}, u32[]{:S(2)}, u32[]{:S(2)}) async-start(bf16[256,1,1,6,4096]{4,3,2,1,0:T(8,128)(2,1)} %bitcast.57), calls=%async_computation.1 | async-start | bytes 33554432 | tf_op jit(solution)/shard_map/all_to_all | solution.py:29
  103.5 0.2 reshape.285
  103.7 364.8 %all-to-all-done.1 = bf16[256,1,1,6,4096]{4,3,2,1,0:T(8,128)(2,1)} async-done(((bf16[256,1,1,6,4096]{4,3,2,1,0:T(8,128)(2,1)}), bf16[256,1,1,6,4096]{4,3,2,1,0:T(8,128)(2,1)}, u32[]{:S(2)}, u32[]{:S(2)}) %all-to-all-start.1) | async-done | bytes 12582944 | tf_op jit(solution)/shard_map/all_to_all | solution.py:29
  468.5 18.8 %reshape_reshape.4 = bf16[1536,4096]{1,0:T(8,128)(2,1)} reshape(bf16[8,32,1,6,4096]{4,3,1,0,2:T(8,128)(2,1)} %bitcast.28) | data formatting | bytes 25165824 | tf_op jit(solution)/shard_map/reshape;reshape | solution.py:93
  487.3 12.6 %convolution_convert_fusion = bf16[501,4096]{1,0:T(8,128)(2,1)} fusion(bf16[1536,4096]{1,0:T(8,128)(2,1)} %reshape_reshape.4, s32[1536]{0:T(1024)S(1)} %fusion.13), kind=kOutput, calls=%fused_computation.7 | convolution fusion | flops 6306860544 | bytes 16693248 | tf_op jit(solution)/shard_map/dot_general | solution.py:97
  (12 shorter events, 0.4 us)
Async XLA Ops:
  9.6 79.0 %all-to-all-start = ((bf16[256,1,1,6,2]{3,4,2,1,0:T(2,128)(2,1)}), bf16[256,1,1,6,2]{3,4,2,1,0:T(2,128)(2,1)S(1)}, u32[]{:S(2)}, u32[]{:S(2)}) async-start(bf16[256,1,1,6,2]{3,4,2,1,0:T(2,128)(2,1)} %copy.21), calls=%async_computation | async-start | bytes 262144 | tf_op jit(solution)/shard_map/all_to_all | solution.py:29
  88.7 379.9 %all-to-all-start.1 = ((bf16[256,1,1,6,4096]{4,3,2,1,0:T(8,128)(2,1)}), bf16[256,1,1,6,4096]{4,3,2,1,0:T(8,128)(2,1)}, u32[]{:S(2)}, u32[]{:S(2)}) async-start(bf16[256,1,1,6,4096]{4,3,2,1,0:T(8,128)(2,1)} %bitcast.57), calls=%async_computation.1 | async-start | bytes 33554432 | tf_op jit(solution)/shard_map/all_to_all | solution.py:29
where the time goes:
time: 501 us; the launch traced here: 500 us
  waiting for transfers between devices  365 us (73%)
  local copies, waits for them, and re-layouts  64.7 us (13%)
  starting transfers between devices  30.4 us (6%)
  other arithmetic  23.5 us (5%)
  matrix products  12.6 us (3%)
    all_to_all x2, waiting for transfers between devices, joined_exchange(): lax.all_to_all(pieces, axis, split_axis=0, concat_axis=0, tiled=True)  365 us
    all_to_all x2, starting transfers between devices, joined_exchange(): lax.all_to_all(pieces, axis, split_axis=0, concat_axis=0, tiled=True)  30.4 us
    scatter x1, local copies, waits for them, and re-layouts, local(): outgoing = jnp.zeros((owner_total * capacity, feature_count), jnp.bfloat1...  19.9 us
    another operation x1, local copies, waits for them, and re-layouts, local(): arrived = arrived.reshape(-1, feature_count)  18.8 us
    another operation x1, local copies, waits for them, and re-layouts, joined_exchange(): pieces = pieces.reshape(-1, *inside)  18.5 us
    dot_general x1, matrix products, local(): jnp.dot(selector, arrived, preferred_element_type=jnp.float32)  12.6 us
  transfers between devices with their start and end apart: 2, of which 1 were waited for; matrix products, arithmetic and copies ran while one was open for 12% of the time, Pallas kernels for 0%

commit v1 on v0

v1 whole, which is shorter than its diff:
```python
import functools

import jax
import jax.numpy as jnp
from jax import lax
from jax.experimental import pallas as pl
from jax.experimental.pallas import tpu as pltpu
from jax.sharding import PartitionSpec as P

VOCAB = 128256
BETA = 0.1
UNITS = 4
WIDTHS = (2048, 2048)
STEPS = 4


def owner_of(ids, row_count):
    return jnp.floor((ids.astype(jnp.float32) + 0.5) * (1.0 / row_count))


def slots_of(ids, row_count, capacity):
    owner = owner_of(ids, row_count)
    tokens = ids.shape[1]
    blocks = tokens // 128
    lower = lax.broadcasted_iota(jnp.int32, (128, 128), 0) < lax.broadcasted_iota(
        jnp.int32, (128, 128), 1
    )
    rows = [owner[:, 128 * b : 128 * b + 128] for b in range(blocks)]
    columns = [jnp.transpose(jnp.broadcast_to(r, (128, 128))) for r in rows]
    ranks = []
    for j in range(blocks):
        hits = jnp.where((columns[j] == rows[j]) & lower, 1.0, 0.0)
        for i in range(j):
            hits = hits + jnp.where(columns[i] == rows[j], 1.0, 0.0)
        ranks.append(jnp.sum(hits, axis=0, keepdims=True))
    rank = jnp.concatenate(ranks, axis=1)
    return (owner * capacity + rank).astype(jnp.int32)


def weight_of(clen, rlen, clogp, rlogp, ref):
    length = clogp.shape[1]
    positions = lax.broadcasted_iota(jnp.int32, (1, length), 1)
    chosen_mask = (positions >= length - clen[0]).astype(jnp.float32)
    rejected_mask = (positions >= length - rlen[0]).astype(jnp.float32)
    chosen = jnp.sum(chosen_mask * clogp[...], axis=1, keepdims=True)
    rejected = jnp.sum(rejected_mask * rlogp[...], axis=1, keepdims=True)
    margin = BETA * ((chosen - ref[0, 0]) - (rejected - ref[1, 0]))
    return BETA * (1.0 / (1.0 + jnp.exp(margin)))


def send_kernel(
    cid, rid, clen, rlen, clogp, rlogp, ref, cg, rg, out, slot, rows, wide, *, row_count, capacity
):
    step = pl.program_id(0)
    half = cg.shape[1]
    height = out.shape[0] // UNITS
    width = out.shape[1]

    @pl.when(step == 0)
    def _():
        ids = jnp.concatenate([cid[...], rid[...]], axis=1)
        slot[...] = slots_of(ids, row_count, capacity)
        weight = weight_of(clen, rlen, clogp, rlogp, ref)
        rows[:half] = (-weight * cg[0].astype(jnp.float32)).astype(jnp.bfloat16)
        rows[half:] = (weight * rg[0].astype(jnp.float32)).astype(jnp.bfloat16)

    place = lax.broadcasted_iota(jnp.int32, (height, 2 * half), 0) + step * height
    pick = jnp.where(place == slot[...], 1.0, 0.0).astype(jnp.bfloat16)
    moved = jnp.dot(pick, rows[...], preferred_element_type=jnp.float32)
    for lane in range(width // 128):
        for u in range(UNITS):
            first = u * width + lane * 128
            wide[lane, pl.ds(u, height, stride=UNITS), :] = moved[:, first : first + 128]
        out[:, lane * 128 : lane * 128 + 128] = wide[lane].astype(jnp.bfloat16)


def label_kernel(cid, rid, out, *, row_count, capacity):
    ids = jnp.concatenate([cid[...], rid[...]], axis=1)
    slot = slots_of(ids, row_count, capacity)
    row = ids - owner_of(ids, row_count).astype(jnp.int32) * row_count
    total = out.shape[0]
    for b in range(0, total, 128):
        place = lax.broadcasted_iota(jnp.int32, (128, ids.shape[1]), 0) + b
        found = jnp.where(place == slot, row - row_count, 0)
        out[b : b + 128] = jnp.sum(found, axis=1, keepdims=True) + row_count


def receive_kernel(label, arrived, *refs):
    out, total, wide = refs[-3:]
    step = pl.program_id(0)
    height = arrived.shape[0] // UNITS

    @pl.when(step == 0)
    def _():
        total[...] = jnp.zeros_like(total)

    lanes = arrived.shape[1] // 128
    for lane in range(lanes):
        wide[lane] = arrived[:, lane * 128 : lane * 128 + 128].astype(jnp.float32)
    pieces = [
        wide[lane, pl.ds(u, height, stride=UNITS), :].astype(jnp.bfloat16)
        for u in range(UNITS)
        for lane in range(lanes)
    ]
    place = lax.broadcasted_iota(jnp.int32, (total.shape[0], height), 0)
    pick = jnp.where(place == label[...], 1.0, 0.0).astype(jnp.bfloat16)
    total[...] += jnp.dot(
        pick, jnp.concatenate(pieces, axis=1), preferred_element_type=jnp.float32
    )

    @pl.when(step == pl.num_programs(0) - 1)
    def _():
        out[...] = total[: out.shape[0]].astype(jnp.bfloat16)


def local(
    chosen_ids,
    rejected_ids,
    chosen_len,
    rejected_len,
    chosen_logp,
    rejected_logp,
    ref_logp,
    chosen_grads,
    rejected_grads,
):
    pair_count, length = chosen_ids.shape
    features = chosen_grads.shape[2]
    owners = lax.axis_size("grp") * lax.axis_size("dp")
    row_count = VOCAB // owners
    capacity = max(2, 3 * pair_count * length // owners)
    slots = owners * capacity
    axes = ("grp", "dp")
    smem = pl.BlockSpec(memory_space=pltpu.SMEM)
    padded = (row_count + 15) // 16 * 16
    sizes = dict(row_count=row_count, capacity=capacity)

    def whole(*shape):
        return pl.BlockSpec(shape, lambda *_: (0,) * len(shape))

    def send(start, size):
        width = size // UNITS
        block = slots * UNITS // STEPS
        grads = pl.BlockSpec((1, length, size), lambda m: (0, 0, start // size))
        return pl.pallas_call(
            functools.partial(send_kernel, **sizes),
            out_shape=jax.ShapeDtypeStruct((slots * UNITS, width), jnp.bfloat16),
            grid=(STEPS,),
            in_specs=[
                whole(1, length),
                whole(1, length),
                smem,
                smem,
                whole(1, length),
                whole(1, length),
                smem,
                grads,
                grads,
            ],
            out_specs=pl.BlockSpec((block, width), lambda m: (m, 0)),
            scratch_shapes=[
                pltpu.VMEM((1, 2 * length), jnp.int32),
                pltpu.VMEM((2 * length, size), jnp.bfloat16),
                pltpu.VMEM((width // 128, block, 128), jnp.float32),
            ],
            name="send",
        )(
            chosen_ids,
            rejected_ids,
            chosen_len,
            rejected_len,
            chosen_logp,
            rejected_logp,
            ref_logp,
            chosen_grads,
            rejected_grads,
        )

    def exchange(array):
        return lax.all_to_all(array, axes, split_axis=0, concat_axis=0, tiled=True)

    def receive(start, size, labels, arrived, table):
        width = size // UNITS
        block = slots * UNITS // STEPS
        operands = [labels, arrived]
        specs = [
            pl.BlockSpec((1, slots // STEPS), lambda k: (0, k)),
            pl.BlockSpec((block, width), lambda k: (k, 0)),
        ]
        aliases = {}
        if table is not None:
            operands.append(table)
            specs.append(pl.BlockSpec(memory_space=pl.ANY))
            aliases = {2: 0}
        return pl.pallas_call(
            receive_kernel,
            out_shape=jax.ShapeDtypeStruct((row_count, features), jnp.bfloat16),
            grid=(STEPS,),
            in_specs=specs,
            out_specs=pl.BlockSpec((row_count, size), lambda k: (0, start // size)),
            scratch_shapes=[
                pltpu.VMEM((padded, size), jnp.float32),
                pltpu.VMEM((width // 128, block, 128), jnp.float32),
            ],
            input_output_aliases=aliases,
            name="receive",
        )(*operands)

    starts = [sum(WIDTHS[:i]) for i in range(len(WIDTHS))]
    arrived = []
    for start, size in zip(starts, WIDTHS):
        sent = send(start, size).reshape(owners, capacity * UNITS, size // UNITS)
        arrived.append(exchange(sent).reshape(slots * UNITS, size // UNITS))
    labels = pl.pallas_call(
        functools.partial(label_kernel, **sizes),
        out_shape=jax.ShapeDtypeStruct((slots, 1), jnp.int32),
        name="label",
    )(chosen_ids, rejected_ids)
    labels = exchange(labels.reshape(owners, capacity)).reshape(1, slots)
    table = None
    for start, size, rows in zip(starts, WIDTHS, arrived):
        table = receive(start, size, labels, rows, table)
    return table


def solution(mesh):
    return jax.shard_map(
        local,
        mesh=mesh,
        in_specs=(
            P(("grp", "dp"), None),
            P(("grp", "dp"), None),
            P(("grp", "dp")),
            P(("grp", "dp")),
            P(("grp", "dp"), None),
            P(("grp", "dp"), None),
            P(None, ("grp", "dp")),
            P(("grp", "dp"), None, None),
            P(("grp", "dp"), None, None),
        ),
        out_specs=P(("grp", "dp"), None),
        check_vma=False,
    )
```

time: 501 us -> 352 us (0.70)
  waiting for transfers between devices: 365 us -> 257 us
  local copies, waits for them, and re-layouts: 64.7 us -> 3.39 us
  Pallas kernels: 0 us -> 48.1 us
  other arithmetic: 23.5 us -> 2.37 us
  matrix products: 12.6 us -> 0 us
  starting transfers between devices: 30.4 us -> 39 us
    all_to_all x2 -> x3, waiting for transfers between devices: 365 us -> 257 us  [exchange(): return lax.all_to_all(array, axes, split_axis=0, concat_axis=0, tiled=True)]
    pallas_call x0 -> x5, Pallas kernels: none -> 48.1 us  [the longest x2 27.1 us: send(): pl.pallas_call(functools.partial(send_kernel, **sizes), out_shape=jax.Sha...]
    another operation x8 -> x0, local copies, waits for them, and re-layouts: 38.8 us -> none  [the longest x1 18.8 us: local(): arrived = arrived.reshape(-1, feature_count)]
    scatter x2 -> x0, local copies, waits for them, and re-layouts: 24.2 us -> none  [the longest x1 19.9 us: local(): outgoing = jnp.zeros((owner_total * capacity, feature_count), jnp.bfloat1...]
    dot_general x1 -> x0, matrix products: 12.6 us -> none  [local(): jnp.dot(selector, arrived, preferred_element_type=jnp.float32)]
    reshape x1 -> x0, other arithmetic: 9.31 us -> none  [local(): chosen_rows.reshape(-1, feature_count)]
    all_to_all x2 -> x3, starting transfers between devices: 30.4 us -> 39 us  [exchange(): return lax.all_to_all(array, axes, split_axis=0, concat_axis=0, tiled=True)]
    concatenate x1 -> x0, other arithmetic: 7.77 us -> none  [local(): jnp.concatenate([chosen_rows.reshape(-1, feature_count), rejected_rows.re...]
  transfers between devices with their start and end apart: 2 -> 3, of which waited for: 1 -> 2; matrix products, arithmetic and copies ran while one was open for 12% -> 1% of each run, Pallas kernels for 0% -> 3%
where the time goes in v1:
time: 352 us; the launch traced here: 351 us
  waiting for transfers between devices  257 us (73%)
  Pallas kernels  48.1 us (14%)
  starting transfers between devices  39 us (11%)
    all_to_all x3, waiting for transfers between devices, exchange(): return lax.all_to_all(array, axes, split_axis=0, concat_axis=0, tiled=True)  257 us
    all_to_all x3, starting transfers between devices, exchange(): return lax.all_to_all(array, axes, split_axis=0, concat_axis=0, tiled=True)  39 us
    pallas_call x2, Pallas kernels, send(): pl.pallas_call(functools.partial(send_kernel, **sizes), out_shape=jax.Sha...  27.1 us
    pallas_call x2, Pallas kernels, receive(): pl.pallas_call(receive_kernel, out_shape=jax.ShapeDtypeStruct((row_count,...  18.2 us
  transfers between devices with their start and end apart: 3, of which 2 were waited for; matrix products, arithmetic and copies ran while one was open for 1% of the time, Pallas kernels for 3%

profile of v1, /device:TPU:1, one launch (start us, length us, event | category | flops | bytes accessed | tf_op | source)
XLA Modules:
  0.0 351.4 jit_solution(16932054416177055395)
XLA Ops:
  0.0 2.8 label.1
  2.8 1.4 reduce
  4.2 0.8 all_to_all.12
  5.1 15.6 %all-to-all-start = ((s32[256,1,6]{2,1,0:T(1,128)}), s32[256,1,6]{2,1,0:T(1,128)S(1)}, u32[]{:S(2)}, u32[]{:S(2)}) async-start(s32[256,1,6]{2,1,0:T(1,128)} %bitcast), calls=%async_computation | async-start | bytes 262144 | tf_op jit(solution)/shard_map/all_to_all | solution.py:180
  22.0 1.3 copy.16.ref
  23.3 13.5 %send.3 = bf16[6144,512]{1,0:T(8,128)(2,1)} custom-call(s32[1,512]{1,0:T(1,128)} %cid.5, s32[1,512]{1,0:T(1,128)} %rid.5, s32[1]{0:T(128)S(6)} %copy.19.clen, s32[1]{0:T(128)S(6)} %copy.20.rlen, f32[1,512]{1,0:T(1,128)} %clogp.3, f32[1,512]{1,0:T(1,128)} %rlogp.3, f32[2,1]{1,0:T(2,128)} %copy.16.ref, bf16[1,512,4096]{2,1,0:T(8,128)(2,1)} %cg.3, ...), custom_call_target="tpu_custom_call" | custom-call | tf_op jit(solution)/shard_map/send/pallas_call | solution.py:145
  36.9 0.0 all-to-all-done
  36.9 14.6 %all-to-all-start.2 = ((bf16[256,24,512]{2,1,0:T(8,128)(2,1)}), bf16[256,24,512]{2,1,0:T(8,128)(2,1)}, u32[]{:S(2)}, u32[]{:S(2)}) async-start(bf16[256,24,512]{2,1,0:T(8,128)(2,1)} %bitcast.6), calls=%async_computation.2 | async-start | bytes 12582912 | tf_op jit(solution)/shard_map/all_to_all | solution.py:180
  51.5 13.5 %send.2 = bf16[6144,512]{1,0:T(8,128)(2,1)} custom-call(s32[1,512]{1,0:T(1,128)} %cid.5, s32[1,512]{1,0:T(1,128)} %rid.5, s32[1]{0:T(128)S(6)} %copy.19.clen, s32[1]{0:T(128)S(6)} %copy.20.rlen, f32[1,512]{1,0:T(1,128)} %clogp.3, f32[1,512]{1,0:T(1,128)} %rlogp.3, f32[2,1]{1,0:T(2,128)} %copy.16.ref, bf16[1,512,4096]{2,1,0:T(8,128)(2,1)} %cg.3, ...), custom_call_target="tpu_custom_call" | custom-call | tf_op jit(solution)/shard_map/send/pallas_call | solution.py:145
  65.0 127.4 %all-to-all-done.2 = bf16[256,24,512]{2,1,0:T(8,128)(2,1)} async-done(((bf16[256,24,512]{2,1,0:T(8,128)(2,1)}), bf16[256,24,512]{2,1,0:T(8,128)(2,1)}, u32[]{:S(2)}, u32[]{:S(2)}) %all-to-all-start.2) | async-done | bytes 6291488 | tf_op jit(solution)/shard_map/all_to_all | solution.py:180
  192.5 8.7 %all-to-all-start.1 = ((bf16[256,24,512]{2,1,0:T(8,128)(2,1)}), bf16[256,24,512]{2,1,0:T(8,128)(2,1)}, u32[]{:S(2)}, u32[]{:S(2)}) async-start(bf16[256,24,512]{2,1,0:T(8,128)(2,1)} %bitcast.5), calls=%async_computation.1 | async-start | bytes 12582912 | tf_op jit(solution)/shard_map/all_to_all | solution.py:180
  201.2 0.5 broadcast.4
  201.7 1.0 reduce.4
  202.7 0.7 reshape.20.label
  203.4 9.1 %receive.2.refs_0_ = bf16[501,4096]{1,0:T(8,128)(2,1)} custom-call(s32[1,1536]{1,0:T(1,128)} %reshape.20.label, bf16[6144,512]{1,0:T(8,128)(2,1)} %bitcast.4.arrived), custom_call_target="tpu_custom_call" | custom-call | tf_op jit(solution)/shard_map/receive/pallas_call | solution.py:195
  212.5 129.8 %all-to-all-done.1 = bf16[256,24,512]{2,1,0:T(8,128)(2,1)} async-done(((bf16[256,24,512]{2,1,0:T(8,128)(2,1)}), bf16[256,24,512]{2,1,0:T(8,128)(2,1)}, u32[]{:S(2)}, u32[]{:S(2)}) %all-to-all-start.1) | async-done | bytes 6291488 | tf_op jit(solution)/shard_map/all_to_all | solution.py:180
  342.3 9.1 %receive.3 = bf16[501,4096]{1,0:T(8,128)(2,1)} custom-call(s32[1,1536]{1,0:T(1,128)} %reshape.20.label, bf16[6144,512]{1,0:T(8,128)(2,1)} %bitcast.2.arrived, bf16[501,4096]{1,0:T(8,128)(2,1)} %receive.2.refs_0_), custom_call_target="tpu_custom_call", output_to_operand_aliasing={{}: (2, {})} | custom-call | tf_op jit(solution)/shard_map/receive/pallas_call | solution.py:195
Async XLA Ops:
  5.1 31.8 %all-to-all-start = ((s32[256,1,6]{2,1,0:T(1,128)}), s32[256,1,6]{2,1,0:T(1,128)S(1)}, u32[]{:S(2)}, u32[]{:S(2)}) async-start(s32[256,1,6]{2,1,0:T(1,128)} %bitcast), calls=%async_computation | async-start | bytes 262144 | tf_op jit(solution)/shard_map/all_to_all | solution.py:180
  36.9 155.6 %all-to-all-start.2 = ((bf16[256,24,512]{2,1,0:T(8,128)(2,1)}), bf16[256,24,512]{2,1,0:T(8,128)(2,1)}, u32[]{:S(2)}, u32[]{:S(2)}) async-start(bf16[256,24,512]{2,1,0:T(8,128)(2,1)} %bitcast.6), calls=%async_computation.2 | async-start | bytes 12582912 | tf_op jit(solution)/shard_map/all_to_all | solution.py:180
  192.5 149.9 %all-to-all-start.1 = ((bf16[256,24,512]{2,1,0:T(8,128)(2,1)}), bf16[256,24,512]{2,1,0:T(8,128)(2,1)}, u32[]{:S(2)}, u32[]{:S(2)}) async-start(bf16[256,24,512]{2,1,0:T(8,128)(2,1)} %bitcast.5), calls=%async_computation.1 | async-start | bytes 12582912 | tf_op jit(solution)/shard_map/all_to_all | solution.py:180
